TPU v7x, 32 devices: a whole 2x2x4 slice. The times are simulated.
32 devices in a mesh: cell: 16 (over z, y, core), band: 2 (over x).
Axes of the slice: x: 2, y: 2, z: 4, core: 2. Of those that a mesh axis runs over, the one named last changes fastest.
Arguments:
- positions: bfloat16 [32, 3, 96, 192], P('cell', None, 'band'), may hold values from -6 to 6
- densities: bfloat16 [32, 3, 96, 192], P('cell', None, 'band'), may hold values from -6 to 6
- operator: bfloat16 [640, 96, 192], P('cell', 'band'), may hold values from -0.046875 to 0.046875
- target_shift: int32 [32, 16], P('cell'), may hold values from 0 to 191
- weights: float32 [640], replicated, may hold values from 0.02 to 0.2
Outputs:
- velocity: float32 [32, 3, 16], P('cell')
All inputs are finite; a program needn't handle non-finite values.
Results may differ from a plain program's by a relative error of at most 0.0003.
Values may be sent and summed in bfloat16 or wider, within the bound.
A program may use at most 64 MiB of HBM per device.

v0:
```python
import jax
import jax.numpy as jnp
from jax import lax
from jax.sharding import PartitionSpec as P

blob_radius = 0.5


def stokes(target, rows, weights):
    spread = target[:, :, :, None] - rows[:, 0:3]
    force = rows[:, 3:6]
    dist_sq = jnp.sum(spread * spread, axis=1)
    along = jnp.sum(spread * force, axis=1)
    blob_sq = blob_radius * blob_radius
    numer = (dist_sq + 2.0 * blob_sq)[:, None] * force + along[:, None] * spread
    kernel = weights / (dist_sq + blob_sq) ** 1.5
    return jnp.sum(numer * kernel[:, None], axis=-1)


def shifted_rows(source, shifts):
    caps_count, comps, lat_count, lon_count = source.shape
    doubled = jnp.concatenate([source, source], axis=3)
    zero = jnp.int32(0)

    def per_capsule(block, capsule_shifts):

        def per_target(offset):
            return lax.dynamic_slice(block, (zero, zero, offset), (comps, lat_count, lon_count))

        return jax.vmap(per_target)(capsule_shifts)

    rolled = jax.vmap(per_capsule)(doubled, shifts)
    rolled = jnp.transpose(rolled, (0, 2, 1, 3, 4))
    return rolled.reshape(caps_count * comps * shifts.shape[1], lat_count * lon_count)


def contract(left, right):
    return lax.dot_general(
        left, right, (((1,), (1,)), ((), ())), preferred_element_type=jnp.float32
    )


def per_device(positions, densities, operator, target_shift, weights):
    source = jnp.concatenate([positions, densities], axis=1)
    caps_here = source.shape[0]
    targets = target_shift.shape[1]
    rows = shifted_rows(source, target_shift)
    piece = lax.all_gather(operator, "cell", axis=0, tiled=True)
    rotated = contract(rows, piece.reshape(piece.shape[0], -1))
    partial_value = rotated.reshape(caps_here, 6, targets, -1)
    summed = lax.psum(partial_value, "band")
    velocity = stokes(summed[:, 0:3, :, 0], summed, weights)
    return velocity


def solution(mesh):
    in_specs = (
        P("cell", None, "band", None),
        P("cell", None, "band", None),
        P("cell", "band", None),
        P("cell", None),
        P(),
    )
    out_specs = P("cell", None, None)
    return jax.shard_map(
        per_device, mesh=mesh, in_specs=in_specs, out_specs=out_specs, check_vma=False
    )
```

profile of v0, /device:TPU:0, one launch (start us, length us, event | category | flops | bytes accessed | tf_op | source)
XLA Modules:
  0.0 182.1 jit_solution(361846499358096142)
XLA Ops:
  6.5 0.0 copy-start.1
  6.5 0.0 all-gather.2.cloned.1.call-start
  6.5 2.5 %copy.14 = bf16[40,48,192]{2,0,1:T(8,128)(2,1)} copy(bf16[40,48,192]{2,1,0:T(8,128)(2,1)} %param.7) | data formatting | bytes 1474560 | tf_op args[2]
  9.1 0.0 all-gather.2.cloned.1.call-update
  9.1 0.0 all-reduce.3.cloned.1.call-start
  9.1 1.3 maximum_maximum_fusion
  10.4 1.2 copy.12
  11.7 0.0 copy-done.1
  11.7 0.1 reshape.15
  11.8 8.6 %gather_fusion = bf16[32,6,48,192]{2,1,3,0:T(8,128)(2,1)} fusion(bf16[2,6,48,384]{2,1,0,3:T(8,128)(2,1)S(1)} %copy.12, s32[32]{0:T(128)S(1)} %reshape.15), kind=kCustom, calls=%fused_computation | custom fusion | bytes 7078400 | tf_op jit(solution)/shard_map/vmap(vmap())/gather | solution.py:28
  20.4 14.0 %copy.13 = bf16[2,16,6,48,192]{4,1,3,2,0:T(8,128)(2,1)} copy(bf16[2,16,6,48,192]{3,2,4,1,0:T(8,128)(2,1)} %bitcast.23) | data formatting | bytes 7077888 | tf_op jit(solution)/shard_map/vmap(vmap())/gather | solution.py:28
  34.4 0.0 copy-start
  34.4 97.8 %all-gather.2.cloned.1.call-done = bf16[640,48,192]{2,0,1:T(8,128)(2,1)} async-done(((bf16[40,48,192]{2,0,1:T(8,128)(2,1)}), bf16[640,48,192]{2,0,1:T(8,128)(2,1)}) %all-gather.2.cloned.1.call-update) | async-done | bytes 11796496 | tf_op jit(solution)/shard_map/all_gather | solution.py:48
  132.2 12.8 %fusion.3 = f32[2,6,16,640]{3,2,1,0:T(8,128)} fusion(bf16[640,48,192]{2,0,1:T(8,128)(2,1)} %all-gather.2.cloned.1.call-done, bf16[2,16,6,48,192]{4,1,3,2,0:T(8,128)(2,1)} %copy.13), kind=kOutput, calls=%fused_computation.4 | convolution fusion | flops 2264924160 | bytes 15826944 | tf_op jit(solution)/shard_map/dot_general | solution.py:38
  145.0 0.0 all-reduce.3.cloned.1.call-update
  145.0 26.2 %all-reduce.3.cloned.1.call-done = f32[2,6,16,640]{3,2,1,0:T(8,128)} async-done(((f32[2,6,16,640]{3,2,1,0:T(8,128)}), f32[2,6,16,640]{3,2,1,0:T(8,128)}) %all-reduce.3.cloned.1.call-update) | async-done | bytes 491536 | tf_op jit(solution)/shard_map/psum | solution.py:51
  171.2 0.8 slice.19
  172.0 0.1 copy.15
  172.1 1.2 multiply_reduce_fusion.1
  173.3 0.0 copy-done
  173.4 1.3 multiply_reduce_fusion
  174.7 0.6 copy.17
  (3 shorter events, 0.1 us)
Async XLA Ops:
  6.5 5.1 %copy-start.1 = (s32[2,16]{1,0:T(2,128)S(1)}, s32[2,16]{1,0:T(2,128)}, u32[]{:S(2)}) copy-start(s32[2,16]{1,0:T(2,128)} %param.8) | copy-start | bytes 388
  6.5 125.7 %all-gather.2.cloned.1.call-start = ((), (), s32[]{:S(2)}) async-start(), calls=%async_computation | async-start | bytes 16711680 | tf_op jit(solution)/shard_map/all_gather | solution.py:48
  9.1 162.2 %all-reduce.3.cloned.1.call-start = ((), (), s32[]{:S(2)}) async-start(), calls=%async_computation.1 | async-start | bytes 983040 | tf_op jit(solution)/shard_map/psum | solution.py:51
  34.4 139.0 %copy-start = (f32[640]{0:T(1024)S(1)}, f32[640]{0:T(1024)}, u32[]{:S(2)}) copy-start(f32[640]{0:T(1024)} %param.9) | copy-start | bytes 7684
Sparse Core Ops, SparseCore 0:
  9.7 122.4 all-gather.1
  145.2 26.0 all-reduce.2
where the time goes:
time: 182 us
  waiting for transfers between devices  124 us (68%)
  local copies, waits for them, and re-layouts  27.9 us (15%)
  between operations  13.5 us (7%)
  matrix products  12.8 us (7%)
  other arithmetic  3.8 us (2%)
    all_gather x1, waiting for transfers between devices, per_device(): piece = lax.all_gather(operator, 'cell', axis=0, tiled=True)  97.8 us
    psum x1, waiting for transfers between devices, per_device(): summed = lax.psum(partial_value, 'band')  26.2 us
    gather x3, local copies, waits for them, and re-layouts, per_target(): lax.dynamic_slice(block, (zero, zero, offset), (comps, lat_count, lon_cou...  22.7 us
    dot_general x1, matrix products, contract(): lax.dot_general(left, right, (((1,), (1,)), ((), ())), preferred_element_...  12.8 us
  transfers between devices with their start and end apart: 2, of which 2 were waited for; matrix products, arithmetic and copies ran while one was open for 14% of the time, Pallas kernels for 0%

commit v1 on v0

--- a/solution.py
+++ b/solution.py
@@ -48,7 +48,7 @@
     piece = lax.all_gather(operator, "cell", axis=0, tiled=True)
     rotated = contract(rows, piece.reshape(piece.shape[0], -1))
     partial_value = rotated.reshape(caps_here, 6, targets, -1)
-    summed = lax.psum(partial_value, "band")
+    summed = jnp.sum(lax.all_gather(partial_value, "band"), axis=0)
     velocity = stokes(summed[:, 0:3, :, 0], summed, weights)
     return velocity
 

time: 182 us -> 167 us (0.918)
  waiting for transfers between devices: 124 us -> 97.9 us
  blocking collectives: 0 us -> 14 us
  other arithmetic: 3.8 us -> 1.75 us
    psum x1 -> x0, waiting for transfers between devices: 26.2 us -> none  [per_device(): summed = lax.psum(partial_value, 'band')]
    all_gather x0 -> x1, blocking collectives: none -> 14 us  [per_device(): summed = jnp.sum(lax.all_gather(partial_value, 'band'), axis=0)]
  transfers between devices with their start and end apart: 2 -> 1, of which waited for: 2 -> 1; matrix products, arithmetic and copies ran while one was open for 14% -> 15% of each run, Pallas kernels for 0% -> 0%
where the time goes in v1:
time: 167 us; the launch traced here: 166 us
  waiting for transfers between devices  97.9 us (59%)
  local copies, waits for them, and re-layouts  27.1 us (16%)
  blocking collectives  14 us (8%)
  between operations  13.5 us (8%)
  matrix products  12 us (7%)
  other arithmetic  1.75 us (1%)
    all_gather x1, waiting for transfers between devices, per_device(): piece = lax.all_gather(operator, 'cell', axis=0, tiled=True)  97.9 us
    gather x3, local copies, waits for them, and re-layouts, per_target(): lax.dynamic_slice(block, (zero, zero, offset), (comps, lat_count, lon_cou...  22.7 us
    all_gather x1, blocking collectives, per_device(): summed = jnp.sum(lax.all_gather(partial_value, 'band'), axis=0)  14 us
    dot_general x1, matrix products, contract(): lax.dot_general(left, right, (((1,), (1,)), ((), ())), preferred_element_...  12 us
  transfers between devices with their start and end apart: 1, of which 1 were waited for; matrix products, arithmetic and copies ran while one was open for 15% of the time, Pallas kernels for 0%

profile of v1, /device:TPU:0, one launch (start us, length us, event | category | flops | bytes accessed | tf_op | source)
XLA Modules:
  0.0 166.3 jit_solution(16971250420751647041)
XLA Ops:
  6.5 0.0 copy-start.1
  6.5 0.0 all-gather.3.cloned.1.call-start
  6.5 2.5 %copy.17 = bf16[40,48,192]{2,0,1:T(8,128)(2,1)} copy(bf16[40,48,192]{2,1,0:T(8,128)(2,1)} %param.7) | data formatting | bytes 1474560 | tf_op args[2]
  9.1 0.0 all-gather.3.cloned.1.call-update
  9.1 1.3 maximum_maximum_fusion
  10.4 1.2 copy.15
  11.6 0.0 copy-done.1
  11.6 0.1 reshape.17
  11.7 8.6 %gather_fusion = bf16[32,6,48,192]{2,1,3,0:T(8,128)(2,1)} fusion(bf16[2,6,48,384]{2,1,0,3:T(8,128)(2,1)S(1)} %copy.15, s32[32]{0:T(128)S(1)} %reshape.17), kind=kCustom, calls=%fused_computation | custom fusion | bytes 7078400 | tf_op jit(solution)/shard_map/vmap(vmap())/gather | solution.py:28
  20.3 14.0 %copy.16 = bf16[2,16,6,48,192]{4,1,3,2,0:T(8,128)(2,1)} copy(bf16[2,16,6,48,192]{3,2,4,1,0:T(8,128)(2,1)} %bitcast.24) | data formatting | bytes 7077888 | tf_op jit(solution)/shard_map/vmap(vmap())/gather | solution.py:28
  34.3 0.0 copy-start
  34.3 97.9 %all-gather.3.cloned.1.call-done = bf16[640,48,192]{2,0,1:T(8,128)(2,1)} async-done(((bf16[40,48,192]{2,0,1:T(8,128)(2,1)}), bf16[640,48,192]{2,0,1:T(8,128)(2,1)}) %all-gather.3.cloned.1.call-update) | async-done | bytes 11796496 | tf_op jit(solution)/shard_map/all_gather | solution.py:48
  132.2 12.0 %fusion.3 = f32[2,6,16,640]{3,2,1,0:T(8,128)S(1)} fusion(bf16[640,48,192]{2,0,1:T(8,128)(2,1)} %all-gather.3.cloned.1.call-done, bf16[2,16,6,48,192]{4,1,3,2,0:T(8,128)(2,1)} %copy.16), kind=kOutput, calls=%fused_computation.4 | convolution fusion | flops 2264924160 | bytes 15826944 | tf_op jit(solution)/shard_map/dot_general | solution.py:38
  144.2 14.0 %all-gather = f32[4,6,16,640]{3,2,1,0:T(8,128)S(1)} all-gather(f32[2,6,16,640]{3,2,1,0:T(8,128)S(1)} %fusion.3), channel_id=2, replica_groups=mesh['cell'=16,'band'=2] {'band'}, dimensions={0}, use_global_device_ids=true | all-gather | bytes 1474560 | tf_op jit(solution)/shard_map/all_gather | solution.py:51
  158.3 0.1 reduce_sum.36
  158.4 0.1 copy.18
  158.5 0.1 multiply_reduce_fusion.1
  158.6 0.0 copy-done
  158.7 0.2 multiply_reduce_fusion
  158.9 0.6 copy.20
  (4 shorter events, 0.1 us)
Async XLA Ops:
  6.5 5.1 %copy-start.1 = (s32[2,16]{1,0:T(2,128)S(1)}, s32[2,16]{1,0:T(2,128)}, u32[]{:S(2)}) copy-start(s32[2,16]{1,0:T(2,128)} %param.8) | copy-start | bytes 388
  6.5 125.7 %all-gather.3.cloned.1.call-start = ((), (), s32[]{:S(2)}) async-start(), calls=%async_computation | async-start | bytes 16711680 | tf_op jit(solution)/shard_map/all_gather | solution.py:48
  34.3 124.3 %copy-start = (f32[640]{0:T(1024)S(1)}, f32[640]{0:T(1024)}, u32[]{:S(2)}) copy-start(f32[640]{0:T(1024)} %param.9) | copy-start | bytes 7684
Sparse Core Ops, SparseCore 0:
  9.7 122.4 all-gather.2
